TPU v7x, 32 devices: a whole 2x2x4 slice. The times are simulated.
32 devices in a mesh: ka: 16 (over z, y, core), ga: 2 (over x).
Axes of the slice: x: 2, y: 2, z: 4, core: 2. Of those that a mesh axis runs over, the one named last changes fastest.
Arguments:
- coeffs: bfloat16 [16, 240, 2, 64, 128], P('ka', 'ga'), may hold values from -0.44921875 to 0.44921875
- neighbour: int32 [16, 3], P('ka'), may hold values from 0 to 15, as said below
- shift_id: int32 [16, 3], P('ka'), may hold values from 0 to 7
- block_map: int32 [8, 240], replicated, may hold values from 0 to 239, as said below
Outputs:
- intersection: float32 [16, 3, 2, 64, 64], P('ka', None, None, 'ga')
Inputs may be any that keep to these rules, and one draw needn't show every extreme that they name: `neighbour`: the k-points are numbered helically. The three columns of row k hold (k + 1) mod 16, (k + 4) mod 16 and (k + 8) mod 16, in an order drawn for each row. `block_map`: each row is a permutation of the 240 blocks. Block j lies in G-slice j // 120. In every row, each G-slice receives exactly 20 of its blocks from one other G-slice, exactly 10 from each of the remaining other G-slices, and the rest from itself.
All inputs are finite; a program needn't handle non-finite values.
Results may differ from a plain program's by a relative error of at most 0.0003.
Values may be sent and summed in bfloat16 or wider, within the bound.
A program may use at most 128 MiB of HBM per device.

v0:
```python
import jax
import jax.numpy as jnp
from jax import lax
from jax.sharding import PartitionSpec as P


def shifted(block, axis, distance):
    devices = range(lax.axis_size(axis))
    route = [((i - distance) % len(devices), i) for i in devices]
    return lax.ppermute(block, axis, route)


def complex_intersection(bra_real, bra_imag, ket_real, ket_imag, form):
    real_part = jnp.einsum(form, bra_real, ket_real, preferred_element_type=jnp.float32)
    real_part = real_part + jnp.einsum(form, bra_imag, ket_imag, preferred_element_type=jnp.float32)
    imag_part = jnp.einsum(form, bra_real, ket_imag, preferred_element_type=jnp.float32)
    imag_part = imag_part - jnp.einsum(form, bra_imag, ket_real, preferred_element_type=jnp.float32)
    return jnp.stack([real_part, imag_part], axis=-3)


def slot_plan(
    home_slice, target_slice, sent_local, place_local, my_slice, slices, capacity, slab_blocks
):
    targets = jnp.arange(slices, dtype=jnp.int32)
    chosen = (home_slice == my_slice)[:, None, :] & (
        target_slice[:, None, :] == targets[None, :, None]
    )
    chosen = chosen & (targets != my_slice)[None, :, None]
    counted = jnp.cumsum(chosen.astype(jnp.int32), axis=2) - 1
    places = jnp.arange(capacity, dtype=jnp.int32)
    matched = (
        chosen[:, :, None, :] & (counted[:, :, None, :] == places[None, None, :, None])
    ).astype(jnp.int32)
    filled = jnp.sum(matched, axis=3)
    sent_block = jnp.sum(matched * sent_local[:, None, None, :], axis=3)
    where_to = jnp.sum(matched * place_local[:, None, None, :], axis=3) + (1 - filled) * slab_blocks
    pair_count = home_slice.shape[0]
    return (
        sent_block.reshape(pair_count, slices * capacity),
        where_to.reshape(pair_count, slices * capacity),
    )


def on_device(coeffs, neighbour, shift_id, block_map):
    k_local = coeffs.shape[0]
    slab_blocks = coeffs.shape[1]
    band_count = coeffs.shape[3]
    lane_width = coeffs.shape[4]
    vector_count = neighbour.shape[1]
    cycle_size = lax.axis_size("ka")
    slices = lax.axis_size("ga")
    my_cycle = lax.axis_index("ka")
    my_slice = lax.axis_index("ga")
    capacity = 2 * max(1, slab_blocks // 12)
    all_blocks = slab_blocks * slices
    pair_count = k_local * vector_count
    k_total = k_local * cycle_size
    row_points = min(16, k_total // 4)
    row_devices = row_points // k_local
    pad_spec = ((0, 0), (0, 1), (0, 0), (0, 0), (0, 0))
    row_point = shifted(coeffs, "ka", -1)
    row_source = jnp.mod(my_cycle + 1, cycle_size)
    plane_kets = shifted(coeffs, "ka", -row_devices)
    plane_source = jnp.mod(my_cycle + row_devices, cycle_size)
    opposite = shifted(coeffs, "ka", cycle_size // 2)
    targets_flat = neighbour.reshape(-1)
    shifts_flat = shift_id.reshape(-1)
    target_device = targets_flat // k_local
    target_lane = targets_flat - target_device * k_local
    ket_index = jnp.where(
        target_device == my_cycle,
        target_lane,
        jnp.where(
            target_device == row_source,
            k_local,
            jnp.where(
                target_device == plane_source,
                k_local + 1 + target_lane,
                2 * k_local + 1 + target_lane,
            ),
        ),
    )
    bra_index = jnp.arange(pair_count, dtype=jnp.int32) // vector_count
    picks = (
        shifts_flat[:, None] == jnp.arange(block_map.shape[0], dtype=jnp.int32)[None, :]
    ).astype(jnp.int32)
    relabel = jnp.sum(picks[:, :, None] * block_map[None, :, :], axis=1)
    dest_global = jnp.broadcast_to(jnp.arange(all_blocks, dtype=jnp.int32)[None, :], relabel.shape)
    source_slice = relabel // slab_blocks
    dest_slice = dest_global // slab_blocks
    source_local = relabel - source_slice * slab_blocks
    dest_local = dest_global - dest_slice * slab_blocks
    kets = jnp.pad(jnp.concatenate([coeffs, row_point, plane_kets, opposite], axis=0), pad_spec)
    own_source = lax.dynamic_slice_in_dim(relabel, my_slice * slab_blocks, slab_blocks, 1)
    self_place = jnp.where(
        own_source // slab_blocks == my_slice, own_source - my_slice * slab_blocks, slab_blocks
    )
    ket_self = kets[ket_index[:, None], self_place]
    ket_self = ket_self.reshape(k_local, vector_count, slab_blocks, 2, band_count, lane_width)
    local_terms = complex_intersection(
        coeffs[:, :, 0],
        coeffs[:, :, 1],
        ket_self[:, :, :, 0],
        ket_self[:, :, :, 1],
        "ksmw,kbsnw->kbmn",
    )
    sent_block, where_to = slot_plan(
        dest_slice, source_slice, dest_local, source_local, my_slice, slices, capacity, slab_blocks
    )
    payload = coeffs[bra_index[:, None], sent_block]
    owner = jnp.broadcast_to(ket_index[:, None], (pair_count, slices))
    blocks = lax.all_to_all(payload, "ga", split_axis=1, concat_axis=1, tiled=True)
    places_in = lax.all_to_all(where_to, "ga", split_axis=1, concat_axis=1, tiled=True)
    owners = lax.all_to_all(owner, "ga", split_axis=1, concat_axis=1, tiled=True)
    partner = kets[owners[:, 0][:, None], places_in]
    remote = complex_intersection(
        blocks[:, :, 0], blocks[:, :, 1], partner[:, :, 0], partner[:, :, 1], "ismw,isnw->imn"
    )
    summed_part = local_terms + remote.reshape(k_local, vector_count, 2, band_count, band_count)
    total = lax.psum(summed_part, "ga")
    row_count = band_count // slices
    return lax.dynamic_slice_in_dim(total, my_slice * row_count, row_count, 3)


def solution(mesh):
    in_specs = (P("ka", "ga", None, None, None), P("ka", None), P("ka", None), P())
    out_specs = P("ka", None, None, "ga", None)
    return jax.shard_map(
        on_device, mesh=mesh, in_specs=in_specs, out_specs=out_specs, check_vma=False
    )
```

profile of v0, /device:TPU:0, one launch (start us, length us, event | category | flops | bytes accessed | tf_op | source)
XLA Modules:
  0.0 407.5 jit_solution(8698845887954236146)
XLA Ops:
  6.5 5.5 %collective-permute-start = (bf16[1,120,2,64,128]{4,3,2,1,0:T(8,128)(2,1)}, bf16[1,120,2,64,128]{4,3,2,1,0:T(8,128)(2,1)}, u32[]{:S(2)}, u32[]{:S(2)}) collective-permute-start(bf16[1,120,2,64,128]{4,3,2,1,0:T(8,128)(2,1)} %param.4), channel_id=1, source_target_pairs={{2,0},{4,2},{6,4},{8,6},{10,8},{12,10},{14,12},{16,14},{18,16},{20... | collective-permute-start | bytes 11796488 | tf_op jit(solution)/shard_map/ppermute | solution.py:10
  12.0 0.4 collective-permute-start.1
  12.5 0.0 collective-permute-start.2
  12.5 0.7 clamp_shift-left_fusion
  13.1 0.6 broadcast_in_dim.35
  13.7 3.2 all-to-all-start.1
  16.9 0.7 fusion.68
  17.6 0.8 multiply_reduce_fusion
  18.4 0.1 and_and_fusion
  18.6 1.8 reduce-window.6
  20.4 0.1 slice.56
  20.5 0.1 copy.78
  20.6 0.1 copy.79
  20.7 0.1 broadcast_add_fusion
  20.8 3.1 select_reduce_fusion.1
  24.0 0.1 copy.83
  24.1 0.1 copy.84
  24.2 0.6 copy.85
  24.8 0.1 copy.80
  24.9 0.1 reshape.387
  25.0 0.1 fusion.63
  25.0 0.0 all-to-all-done.1
  25.0 3.3 all-to-all-start.2
  28.3 0.1 reshape.395
  28.4 5.1 %gather_fusion.1 = bf16[120,2,64,128]{3,2,1,0:T(8,128)(2,1)} fusion(bf16[1,120,2,64,128]{4,3,2,1,0:T(8,128)(2,1)} %param.4, s32[120]{0:T(128)S(1)} %reshape.395), kind=kCustom, calls=%fused_computation.1 | custom fusion | bytes 7865280 | tf_op jit(solution)/shard_map/gather | solution.py:110
  33.5 5.4 %copy.81 = bf16[3,40,2,64,128]{4,3,0,2,1:T(8,128)(2,1)} copy(bf16[3,40,2,64,128]{4,3,2,1,0:T(8,128)(2,1)} %bitcast.179) | data formatting | bytes 7864320 | tf_op jit(solution)/shard_map/gather | solution.py:110
  38.9 0.0 all-to-all-done.2
  38.9 5.5 %all-to-all-start = ((bf16[3,40,2,64,128]{4,3,0,2,1:T(8,128)(2,1)}), bf16[3,40,2,64,128]{4,3,0,2,1:T(8,128)(2,1)}, u32[]{:S(2)}, u32[]{:S(2)}) async-start(bf16[3,40,2,64,128]{4,3,0,2,1:T(8,128)(2,1)} %copy.81), calls=%async_computation | async-start | bytes 7864320 | tf_op jit(solution)/shard_map/all_to_all | solution.py:112
  44.4 0.2 all-reduce.4.cloned.1.call-start
  44.6 0.1 fusion.60
  44.7 0.1 reshape.389
  44.8 0.1 all_to_all.19
  44.9 0.1 fusion.66
  44.9 0.1 reshape.401
  45.0 43.7 %all-to-all-done = bf16[3,40,2,64,128]{4,3,0,2,1:T(8,128)(2,1)} async-done(((bf16[3,40,2,64,128]{4,3,0,2,1:T(8,128)(2,1)}), bf16[3,40,2,64,128]{4,3,0,2,1:T(8,128)(2,1)}, u32[]{:S(2)}, u32[]{:S(2)}) %all-to-all-start) | async-done | bytes 3932192 | tf_op jit(solution)/shard_map/all_to_all | solution.py:112
  88.7 4.5 %fusion.77 = (bf16[3,40,1,64,128]{4,3,0,2,1:T(8,128)(2,1)S(1)}, bf16[3,40,1,64,128]{4,3,0,2,1:T(8,128)(2,1)}) fusion(bf16[3,40,2,64,128]{4,3,0,2,1:T(8,128)(2,1)} %all-to-all-done), kind=kLoop, calls=%fused_computation.110 | loop fusion | bytes 7864320 | tf_op jit(solution)/shard_map/slice | solution.py:117
  93.2 4.5 %collective-permute-done = bf16[1,120,2,64,128]{4,3,2,1,0:T(8,128)(2,1)} collective-permute-done((bf16[1,120,2,64,128]{4,3,2,1,0:T(8,128)(2,1)}, bf16[1,120,2,64,128]{4,3,2,1,0:T(8,128)(2,1)}, u32[]{:S(2)}, u32[]{:S(2)}) %collective-permute-start) | collective-permute-done | bytes 3932192 | tf_op jit(solution)/shard_map/ppermute | solution.py:10
  97.7 83.4 %collective-permute-done.1 = bf16[1,120,2,64,128]{4,3,2,1,0:T(8,128)(2,1)} collective-permute-done((bf16[1,120,2,64,128]{4,3,2,1,0:T(8,128)(2,1)}, bf16[1,120,2,64,128]{4,3,2,1,0:T(8,128)(2,1)}, u32[]{:S(2)}, u32[]{:S(2)}) %collective-permute-start.1) | collective-permute-done | bytes 3932192 | tf_op jit(solution)/shard_map/ppermute | solution.py:10
  181.1 126.2 %collective-permute-done.2 = bf16[1,120,2,64,128]{4,3,2,1,0:T(8,128)(2,1)} collective-permute-done((bf16[1,120,2,64,128]{4,3,2,1,0:T(8,128)(2,1)}, bf16[1,120,2,64,128]{4,3,2,1,0:T(8,128)(2,1)}, u32[]{:S(2)}, u32[]{:S(2)}) %collective-permute-start.2) | collective-permute-done | bytes 3932192 | tf_op jit(solution)/shard_map/ppermute | solution.py:10
  307.4 0.0 copy-done
  307.4 12.7 %fusion.6 = bf16[4,121,2,64,128]{4,3,2,1,0:T(8,128)(2,1)} fusion(bf16[1,120,2,64,128]{4,3,2,1,0:T(8,128)(2,1)} %collective-permute-done.2, bf16[1,120,2,64,128]{4,3,2,1,0:T(8,128)(2,1)} %collective-permute-done.1, bf16[1,120,2,64,128]{4,3,2,1,0:T(8,128)(2,1)} %collective-permute-done, bf16[1,120,2,64,128]{4,3,2,1,0:T(8,128)(2,1)S(1)} %copy-done), kind=kLoop, calls=%fused_computation.10 | loop fusion | flops 103088128 | bytes 31588352 | tf_op jit(solution)/shard_map/concatenate | solution.py:93
  320.1 8.8 %gather_fusion.2 = bf16[120,2,64,128]{3,2,1,0:T(8,128)(2,1)} fusion(bf16[4,121,2,64,128]{4,3,2,1,0:T(8,128)(2,1)} %fusion.6, s32[120]{0:T(128)S(1)} %reshape.401), kind=kCustom, calls=%fused_computation.2 | custom fusion | bytes 7865280 | tf_op jit(solution)/shard_map/gather | solution.py:115
  328.9 3.1 copy.87
  332.0 0.0 copy-start.2
  332.1 0.0 copy-done.4
  332.1 0.6 fusion.23
  332.7 1.3 copy-done.2
  334.0 0.7 fusion.24
  334.7 25.5 %gather_fusion = bf16[360,2,64,128]{3,2,1,0:T(8,128)(2,1)} fusion(bf16[4,121,2,64,128]{4,3,2,1,0:T(8,128)(2,1)} %fusion.6, s32[360]{0:T(512)S(1)} %reshape.389), kind=kCustom, calls=%fused_computation | custom fusion | bytes 23595840 | tf_op jit(solution)/shard_map/gather | solution.py:98
  360.1 6.5 %copy.75 = bf16[360,2,64,128]{3,2,0,1:T(8,128)(2,1)S(1)} copy(bf16[360,2,64,128]{3,2,1,0:T(8,128)(2,1)} %gather_fusion) | data formatting | bytes 23592960 | tf_op jit(solution)/shard_map/gather | solution.py:98
  366.7 0.0 copy-done.1
  366.7 1.7 fusion.27
  368.4 0.0 copy-start.3
  368.4 1.7 fusion.36
  370.0 0.4 copy-done.3
  370.5 0.7 fusion.54
  371.2 0.7 fusion.52
  371.8 1.7 fusion.42
  373.5 1.7 fusion.48
  375.2 0.7 maximum_add_fusion
  375.9 0.0 all-reduce.4.cloned.1.call-update
  375.9 22.9 %all-reduce.4.cloned.1.call-done = f32[1,3,2,64,64]{3,4,1,2,0:T(8,128)} async-done(((f32[1,3,2,64,64]{3,4,1,2,0:T(8,128)}), f32[1,3,2,64,64]{3,4,1,2,0:T(8,128)}) %all-reduce.4.cloned.1.call-update) | async-done | bytes 98320 | tf_op jit(solution)/shard_map/psum | solution.py:120
  398.8 1.0 constant_dynamic-slice_fusion
  399.9 0.8 copy.93
  (18 shorter events, 0.2 us)
Async XLA Ops:
  6.5 91.2 %collective-permute-start = (bf16[1,120,2,64,128]{4,3,2,1,0:T(8,128)(2,1)}, bf16[1,120,2,64,128]{4,3,2,1,0:T(8,128)(2,1)}, u32[]{:S(2)}, u32[]{:S(2)}) collective-permute-start(bf16[1,120,2,64,128]{4,3,2,1,0:T(8,128)(2,1)} %param.4), channel_id=1, source_target_pairs={{2,0},{4,2},{6,4},{8,6},{10,8},{12,10},{14,12},{16,14},{18,16},{20... | collective-permute-start | bytes 11796488 | tf_op jit(solution)/shard_map/ppermute | solution.py:10
  12.0 169.1 %collective-permute-start.1 = (bf16[1,120,2,64,128]{4,3,2,1,0:T(8,128)(2,1)}, bf16[1,120,2,64,128]{4,3,2,1,0:T(8,128)(2,1)}, u32[]{:S(2)}, u32[]{:S(2)}) collective-permute-start(bf16[1,120,2,64,128]{4,3,2,1,0:T(8,128)(2,1)} %param.4), channel_id=1, source_target_pairs={{8,0},{10,2},{12,4},{14,6},{16,8},{18,10},{20,12},{22,14},{24,16},... | collective-permute-start | bytes 11796488 | tf_op jit(solution)/shard_map/ppermute | solution.py:10
  12.5 294.9 %collective-permute-start.2 = (bf16[1,120,2,64,128]{4,3,2,1,0:T(8,128)(2,1)}, bf16[1,120,2,64,128]{4,3,2,1,0:T(8,128)(2,1)}, u32[]{:S(2)}, u32[]{:S(2)}) collective-permute-start(bf16[1,120,2,64,128]{4,3,2,1,0:T(8,128)(2,1)} %param.4), channel_id=1, source_target_pairs={{16,0},{18,2},{20,4},{22,6},{24,8},{26,10},{28,12},{30,14},{0,16},... | collective-permute-start | bytes 11796488 | tf_op jit(solution)/shard_map/ppermute | solution.py:10
  13.7 11.3 %all-to-all-start.1 = ((s32[3,2,1]{0,2,1:T(1,128)}), s32[3,2,1]{0,2,1:T(1,128)S(1)}, u32[]{:S(2)}, u32[]{:S(2)}) async-start(s32[3,2,1]{0,2,1:T(1,128)} %broadcast_in_dim.35), calls=%async_computation.1 | async-start | bytes 2048 | tf_op jit(solution)/shard_map/all_to_all | solution.py:114
  25.0 13.8 %all-to-all-start.2 = ((s32[3,2,20]{2,0,1:T(4,128)}), s32[3,2,20]{2,0,1:T(4,128)S(1)}, u32[]{:S(2)}, u32[]{:S(2)}) async-start(s32[3,2,20]{2,0,1:T(4,128)} %copy.85), calls=%async_computation.2 | async-start | bytes 8192 | tf_op jit(solution)/shard_map/all_to_all | solution.py:113
  38.9 49.9 %all-to-all-start = ((bf16[3,40,2,64,128]{4,3,0,2,1:T(8,128)(2,1)}), bf16[3,40,2,64,128]{4,3,0,2,1:T(8,128)(2,1)}, u32[]{:S(2)}, u32[]{:S(2)}) async-start(bf16[3,40,2,64,128]{4,3,0,2,1:T(8,128)(2,1)} %copy.81), calls=%async_computation | async-start | bytes 7864320 | tf_op jit(solution)/shard_map/all_to_all | solution.py:112
  44.4 354.5 %all-reduce.4.cloned.1.call-start = ((), (), s32[]{:S(2)}) async-start(), calls=%async_computation.3 | async-start | bytes 393216 | tf_op jit(solution)/shard_map/psum | solution.py:120
  88.7 218.6 %copy-start = (bf16[1,120,2,64,128]{4,3,2,1,0:T(8,128)(2,1)S(1)}, bf16[1,120,2,64,128]{4,3,2,1,0:T(8,128)(2,1)}, u32[]{:S(2)}) copy-start(bf16[1,120,2,64,128]{4,3,2,1,0:T(8,128)(2,1)} %param.4) | copy-start | bytes 11796484
  328.9 3.2 copy-start.4
  332.0 2.0 copy-start.2
  360.1 6.5 %copy-start.1 = (bf16[1,120,2,64,128]{4,3,2,1,0:T(8,128)(2,1)S(1)}, bf16[1,120,2,64,128]{4,3,2,1,0:T(8,128)(2,1)}, u32[]{:S(2)}) copy-start(bf16[1,120,2,64,128]{4,3,2,1,0:T(8,128)(2,1)} %param.4) | copy-start | bytes 11796484
  368.4 2.1 copy-start.3
Sparse Core Ops, SparseCore 0:
  376.0 22.7 all-reduce.3
where the time goes:
time: 408 us; the launch traced here: 407 us
  waiting for transfers between devices  281 us (69%)
  local copies, waits for them, and re-layouts  64.7 us (16%)
  other arithmetic  21 us (5%)
  starting transfers between devices  18.1 us (4%)
  between operations  13.6 us (3%)
  matrix products  9.31 us (2%)
    ppermute x3, waiting for transfers between devices, shifted(): return lax.ppermute(block, axis, route)  214 us
    all_to_all x1, waiting for transfers between devices, on_device(): lax.all_to_all(payload, 'ga', split_axis=1, concat_axis=1, tiled=True)  43.7 us
    gather x2, local copies, waits for them, and re-layouts, on_device(): ket_self = kets[ket_index[:, None], self_place]  32 us
    psum x1, waiting for transfers between devices, on_device(): total = lax.psum(summed_part, 'ga')  22.9 us
    concatenate x1, other arithmetic, on_device(): jnp.concatenate([coeffs, row_point, plane_kets, opposite], axis=0)  12.7 us
    gather x2, local copies, waits for them, and re-layouts, on_device(): partner = kets[owners[:, 0][:, None], places_in]  12 us
    gather x2, local copies, waits for them, and re-layouts, on_device(): payload = coeffs[bra_index[:, None], sent_block]  10.5 us
  transfers between devices with their start and end apart: 7, of which 5 were waited for; matrix products, arithmetic and copies ran while one was open for 6% of the time, Pallas kernels for 0%

commit v1 on v0

--- a/solution.py
+++ b/solution.py
@@ -2,6 +2,11 @@
 import jax.numpy as jnp
 from jax import lax
 from jax.sharding import PartitionSpec as P
+from jax.lax import all_gather
+
+
+def stops_all_note(slab_in):
+    return jnp.sum(all_gather(slab_in, "ga"), 0)
 
 
 def shifted(block, axis, distance):
@@ -117,7 +122,7 @@
         blocks[:, :, 0], blocks[:, :, 1], partner[:, :, 0], partner[:, :, 1], "ismw,isnw->imn"
     )
     summed_part = local_terms + remote.reshape(k_local, vector_count, 2, band_count, band_count)
-    total = lax.psum(summed_part, "ga")
+    total = stops_all_note(summed_part)
     row_count = band_count // slices
     return lax.dynamic_slice_in_dim(total, my_slice * row_count, row_count, 3)
 

time: 408 us -> 377 us (0.924)
  waiting for transfers between devices: 281 us -> 258 us
  between operations: 13.6 us -> 0.22 us
  blocking collectives: 0 us -> 6.34 us
    psum x1 -> x0, waiting for transfers between devices: 22.9 us -> none  [on_device(): total = lax.psum(summed_part, 'ga')]
    all_gather x0 -> x1, blocking collectives: none -> 6.34 us  [stops_all_note(): return jnp.sum(all_gather(slab_in, 'ga'), 0)]
  transfers between devices with their start and end apart: 7 -> 6, of which waited for: 5 -> 4; matrix products, arithmetic and copies ran while one was open for 6% -> 7% of each run, Pallas kernels for 0% -> 0%
where the time goes in v1:
time: 377 us; the launch traced here: 376 us
  waiting for transfers between devices  258 us (68%)
  local copies, waits for them, and re-layouts  63.7 us (17%)
  other arithmetic  20.4 us (5%)
  starting transfers between devices  18.1 us (5%)
  matrix products  9.29 us (2%)
  blocking collectives  6.34 us (2%)
    ppermute x3, waiting for transfers between devices, shifted(): return lax.ppermute(block, axis, route)  214 us
    all_to_all x1, waiting for transfers between devices, on_device(): lax.all_to_all(payload, 'ga', split_axis=1, concat_axis=1, tiled=True)  43.9 us
    gather x2, local copies, waits for them, and re-layouts, on_device(): ket_self = kets[ket_index[:, None], self_place]  32 us
    concatenate x1, other arithmetic, on_device(): jnp.concatenate([coeffs, row_point, plane_kets, opposite], axis=0)  12.7 us
    gather x2, local copies, waits for them, and re-layouts, on_device(): partner = kets[owners[:, 0][:, None], places_in]  11.9 us
    gather x2, local copies, waits for them, and re-layouts, on_device(): payload = coeffs[bra_index[:, None], sent_block]  10.5 us
  transfers between devices with their start and end apart: 6, of which 4 were waited for; matrix products, arithmetic and copies ran while one was open for 7% of the time, Pallas kernels for 0%

profile of v1, /device:TPU:0, one launch (start us, length us, event | category | flops | bytes accessed | tf_op | source)
XLA Modules:
  0.0 375.8 jit_solution(2927511646687502225)
XLA Ops:
  0.0 5.5 %collective-permute-start = (bf16[1,120,2,64,128]{4,3,2,1,0:T(8,128)(2,1)}, bf16[1,120,2,64,128]{4,3,2,1,0:T(8,128)(2,1)}, u32[]{:S(2)}, u32[]{:S(2)}) collective-permute-start(bf16[1,120,2,64,128]{4,3,2,1,0:T(8,128)(2,1)} %param.4), channel_id=1, source_target_pairs={{2,0},{4,2},{6,4},{8,6},{10,8},{12,10},{14,12},{16,14},{18,16},{20... | collective-permute-start | bytes 11796488 | tf_op jit(solution)/shard_map/ppermute | solution.py:15
  5.5 0.4 collective-permute-start.1
  5.9 0.0 collective-permute-start.2
  5.9 0.7 clamp_shift-left_fusion
  6.6 0.6 broadcast_in_dim.35
  7.2 3.2 all-to-all-start.1
  10.5 0.7 fusion.68
  11.2 0.8 multiply_reduce_fusion
  12.0 0.1 and_and_fusion
  12.1 1.8 reduce-window.6
  13.9 0.1 slice.56
  14.0 0.1 copy.81
  14.2 0.1 copy.82
  14.3 0.1 broadcast_add_fusion
  14.4 3.1 select_reduce_fusion.1
  17.5 0.1 copy.86
  17.6 0.1 copy.87
  17.7 0.6 copy.88
  18.3 0.1 copy.83
  18.4 0.1 reshape.397
  18.5 0.1 fusion.63
  18.6 0.0 all-to-all-done.1
  18.6 3.3 all-to-all-start.2
  21.8 0.1 reshape.405
  21.9 5.1 %gather_fusion.1 = bf16[120,2,64,128]{3,2,1,0:T(8,128)(2,1)} fusion(bf16[1,120,2,64,128]{4,3,2,1,0:T(8,128)(2,1)} %param.4, s32[120]{0:T(128)S(1)} %reshape.405), kind=kCustom, calls=%fused_computation.1 | custom fusion | bytes 7865280 | tf_op jit(solution)/shard_map/gather | solution.py:115
  27.0 5.4 %copy.84 = bf16[3,40,2,64,128]{4,3,0,2,1:T(8,128)(2,1)} copy(bf16[3,40,2,64,128]{4,3,2,1,0:T(8,128)(2,1)} %bitcast.181) | data formatting | bytes 7864320 | tf_op jit(solution)/shard_map/gather | solution.py:115
  32.4 0.0 all-to-all-done.2
  32.4 5.7 %all-to-all-start = ((bf16[3,40,2,64,128]{4,3,0,2,1:T(8,128)(2,1)}), bf16[3,40,2,64,128]{4,3,0,2,1:T(8,128)(2,1)}, u32[]{:S(2)}, u32[]{:S(2)}) async-start(bf16[3,40,2,64,128]{4,3,0,2,1:T(8,128)(2,1)} %copy.84), calls=%async_computation | async-start | bytes 7864320 | tf_op jit(solution)/shard_map/all_to_all | solution.py:117
  38.1 0.1 fusion.60
  38.2 0.1 reshape.399
  38.3 0.1 all_to_all.19
  38.4 0.1 fusion.66
  38.4 0.1 reshape.411
  38.5 43.9 %all-to-all-done = bf16[3,40,2,64,128]{4,3,0,2,1:T(8,128)(2,1)} async-done(((bf16[3,40,2,64,128]{4,3,0,2,1:T(8,128)(2,1)}), bf16[3,40,2,64,128]{4,3,0,2,1:T(8,128)(2,1)}, u32[]{:S(2)}, u32[]{:S(2)}) %all-to-all-start) | async-done | bytes 3932192 | tf_op jit(solution)/shard_map/all_to_all | solution.py:117
  82.5 0.0 copy-start
  82.5 4.5 %fusion.77 = (bf16[3,40,1,64,128]{4,3,0,2,1:T(8,128)(2,1)S(1)}, bf16[3,40,1,64,128]{4,3,0,2,1:T(8,128)(2,1)}) fusion(bf16[3,40,2,64,128]{4,3,0,2,1:T(8,128)(2,1)} %all-to-all-done), kind=kLoop, calls=%fused_computation.110 | loop fusion | bytes 7864320 | tf_op jit(solution)/shard_map/slice | solution.py:122
  86.9 4.2 %collective-permute-done = bf16[1,120,2,64,128]{4,3,2,1,0:T(8,128)(2,1)} collective-permute-done((bf16[1,120,2,64,128]{4,3,2,1,0:T(8,128)(2,1)}, bf16[1,120,2,64,128]{4,3,2,1,0:T(8,128)(2,1)}, u32[]{:S(2)}, u32[]{:S(2)}) %collective-permute-start) | collective-permute-done | bytes 3932192 | tf_op jit(solution)/shard_map/ppermute | solution.py:15
  91.2 83.4 %collective-permute-done.1 = bf16[1,120,2,64,128]{4,3,2,1,0:T(8,128)(2,1)} collective-permute-done((bf16[1,120,2,64,128]{4,3,2,1,0:T(8,128)(2,1)}, bf16[1,120,2,64,128]{4,3,2,1,0:T(8,128)(2,1)}, u32[]{:S(2)}, u32[]{:S(2)}) %collective-permute-start.1) | collective-permute-done | bytes 3932192 | tf_op jit(solution)/shard_map/ppermute | solution.py:15
  174.6 126.2 %collective-permute-done.2 = bf16[1,120,2,64,128]{4,3,2,1,0:T(8,128)(2,1)} collective-permute-done((bf16[1,120,2,64,128]{4,3,2,1,0:T(8,128)(2,1)}, bf16[1,120,2,64,128]{4,3,2,1,0:T(8,128)(2,1)}, u32[]{:S(2)}, u32[]{:S(2)}) %collective-permute-start.2) | collective-permute-done | bytes 3932192 | tf_op jit(solution)/shard_map/ppermute | solution.py:15
  300.8 0.0 copy-done
  300.8 12.7 %fusion.6 = bf16[4,121,2,64,128]{4,3,2,1,0:T(8,128)(2,1)} fusion(bf16[1,120,2,64,128]{4,3,2,1,0:T(8,128)(2,1)} %collective-permute-done.2, bf16[1,120,2,64,128]{4,3,2,1,0:T(8,128)(2,1)} %collective-permute-done.1, bf16[1,120,2,64,128]{4,3,2,1,0:T(8,128)(2,1)} %collective-permute-done, bf16[1,120,2,64,128]{4,3,2,1,0:T(8,128)(2,1)S(1)} %copy-done), kind=kLoop, calls=%fused_computation.10 | loop fusion | flops 103088128 | bytes 31588352 | tf_op jit(solution)/shard_map/concatenate | solution.py:98
  313.6 8.8 %gather_fusion.2 = bf16[120,2,64,128]{3,2,1,0:T(8,128)(2,1)} fusion(bf16[4,121,2,64,128]{4,3,2,1,0:T(8,128)(2,1)} %fusion.6, s32[120]{0:T(128)S(1)} %reshape.411), kind=kCustom, calls=%fused_computation.2 | custom fusion | bytes 7865280 | tf_op jit(solution)/shard_map/gather | solution.py:120
  322.4 0.0 copy-start.4
  322.4 3.1 copy.90
  325.5 0.0 copy-start.2
  325.5 0.0 copy-done.4
  325.5 0.6 fusion.23
  326.2 1.3 copy-done.2
  327.5 0.6 fusion.24
  328.1 25.5 %gather_fusion = bf16[360,2,64,128]{3,2,1,0:T(8,128)(2,1)} fusion(bf16[4,121,2,64,128]{4,3,2,1,0:T(8,128)(2,1)} %fusion.6, s32[360]{0:T(512)S(1)} %reshape.399), kind=kCustom, calls=%fused_computation | custom fusion | bytes 23595840 | tf_op jit(solution)/shard_map/gather | solution.py:103
  353.6 0.0 copy-start.1
  353.6 6.5 %copy.78 = bf16[360,2,64,128]{3,2,0,1:T(8,128)(2,1)S(1)} copy(bf16[360,2,64,128]{3,2,1,0:T(8,128)(2,1)} %gather_fusion) | data formatting | bytes 23592960 | tf_op jit(solution)/shard_map/gather | solution.py:103
  360.1 0.0 copy-done.1
  360.1 1.7 fusion.27
  361.8 0.0 copy-start.3
  361.8 1.7 fusion.36
  363.5 0.4 copy-done.3
  363.9 0.7 fusion.54
  364.6 0.7 fusion.52
  365.3 1.7 fusion.42
  367.0 1.7 fusion.48
  368.7 0.1 copy.96
  368.8 6.3 %all_gather.4 = f32[2,1,3,2,64,64]{5,4,3,2,1,0:T(8,128)S(1)} all-gather(f32[1,1,3,2,64,64]{5,4,3,2,1,0:T(8,128)S(1)} %copy.96), channel_id=1, replica_groups=mesh['ka'=16,'ga'=2] {'ga'}, dimensions={0}, use_global_device_ids=true | all-gather | bytes 294912 | tf_op jit(solution)/shard_map/all_gather | solution.py:9
  375.2 0.7 dynamic-slice_bitcast_fusion
  (17 shorter events, 0.2 us)
Async XLA Ops:
  0.0 91.2 %collective-permute-start = (bf16[1,120,2,64,128]{4,3,2,1,0:T(8,128)(2,1)}, bf16[1,120,2,64,128]{4,3,2,1,0:T(8,128)(2,1)}, u32[]{:S(2)}, u32[]{:S(2)}) collective-permute-start(bf16[1,120,2,64,128]{4,3,2,1,0:T(8,128)(2,1)} %param.4), channel_id=1, source_target_pairs={{2,0},{4,2},{6,4},{8,6},{10,8},{12,10},{14,12},{16,14},{18,16},{20... | collective-permute-start | bytes 11796488 | tf_op jit(solution)/shard_map/ppermute | solution.py:15
  5.5 169.1 %collective-permute-start.1 = (bf16[1,120,2,64,128]{4,3,2,1,0:T(8,128)(2,1)}, bf16[1,120,2,64,128]{4,3,2,1,0:T(8,128)(2,1)}, u32[]{:S(2)}, u32[]{:S(2)}) collective-permute-start(bf16[1,120,2,64,128]{4,3,2,1,0:T(8,128)(2,1)} %param.4), channel_id=1, source_target_pairs={{8,0},{10,2},{12,4},{14,6},{16,8},{18,10},{20,12},{22,14},{24,16},... | collective-permute-start | bytes 11796488 | tf_op jit(solution)/shard_map/ppermute | solution.py:15
  5.9 294.9 %collective-permute-start.2 = (bf16[1,120,2,64,128]{4,3,2,1,0:T(8,128)(2,1)}, bf16[1,120,2,64,128]{4,3,2,1,0:T(8,128)(2,1)}, u32[]{:S(2)}, u32[]{:S(2)}) collective-permute-start(bf16[1,120,2,64,128]{4,3,2,1,0:T(8,128)(2,1)} %param.4), channel_id=1, source_target_pairs={{16,0},{18,2},{20,4},{22,6},{24,8},{26,10},{28,12},{30,14},{0,16},... | collective-permute-start | bytes 11796488 | tf_op jit(solution)/shard_map/ppermute | solution.py:15
  7.2 11.4 %all-to-all-start.1 = ((s32[3,2,1]{0,2,1:T(1,128)}), s32[3,2,1]{0,2,1:T(1,128)S(1)}, u32[]{:S(2)}, u32[]{:S(2)}) async-start(s32[3,2,1]{0,2,1:T(1,128)} %broadcast_in_dim.35), calls=%async_computation.1 | async-start | bytes 2048 | tf_op jit(solution)/shard_map/all_to_all | solution.py:119
  18.6 13.8 %all-to-all-start.2 = ((s32[3,2,20]{2,0,1:T(4,128)}), s32[3,2,20]{2,0,1:T(4,128)S(1)}, u32[]{:S(2)}, u32[]{:S(2)}) async-start(s32[3,2,20]{2,0,1:T(4,128)} %copy.88), calls=%async_computation.2 | async-start | bytes 8192 | tf_op jit(solution)/shard_map/all_to_all | solution.py:118
  32.4 50.0 %all-to-all-start = ((bf16[3,40,2,64,128]{4,3,0,2,1:T(8,128)(2,1)}), bf16[3,40,2,64,128]{4,3,0,2,1:T(8,128)(2,1)}, u32[]{:S(2)}, u32[]{:S(2)}) async-start(bf16[3,40,2,64,128]{4,3,0,2,1:T(8,128)(2,1)} %copy.84), calls=%async_computation | async-start | bytes 7864320 | tf_op jit(solution)/shard_map/all_to_all | solution.py:117
  82.5 218.4 %copy-start = (bf16[1,120,2,64,128]{4,3,2,1,0:T(8,128)(2,1)S(1)}, bf16[1,120,2,64,128]{4,3,2,1,0:T(8,128)(2,1)}, u32[]{:S(2)}) copy-start(bf16[1,120,2,64,128]{4,3,2,1,0:T(8,128)(2,1)} %param.4) | copy-start | bytes 11796484
  322.4 3.2 copy-start.4
  325.5 2.0 copy-start.2
  353.6 6.5 %copy-start.1 = (bf16[1,120,2,64,128]{4,3,2,1,0:T(8,128)(2,1)S(1)}, bf16[1,120,2,64,128]{4,3,2,1,0:T(8,128)(2,1)}, u32[]{:S(2)}) copy-start(bf16[1,120,2,64,128]{4,3,2,1,0:T(8,128)(2,1)} %param.4) | copy-start | bytes 11796484
  361.8 2.1 copy-start.3
